TPU v7x, 32 devices: a whole 2x2x4 slice. The times are simulated.
32 devices in a mesh: rep: 1, r: 4 (over z), s: 8 (over x, y, core).
Axes of the slice: x: 2, y: 2, z: 4, core: 2. Of those that a mesh axis runs over, the one named last changes fastest.
Arguments:
- x: bfloat16 [32, 4096, 512], P(('rep', 'r', 's'))
- dy: bfloat16 [32, 4096, 512], P(('rep', 'r', 's'))
- w_gate: bfloat16 [2, 512, 4096], P(None, 's')
- w_up: bfloat16 [2, 512, 4096], P(None, 's')
- w_down: bfloat16 [2, 4096, 512], P(None, 's')
- m_w_gate: float32 [2, 512, 4096], P(None, 's')
- m_w_up: float32 [2, 512, 4096], P(None, 's')
- m_w_down: float32 [2, 4096, 512], P(None, 's')
- v_w_gate: float32 [2, 512, 4096], P(None, 's')
- v_w_up: float32 [2, 512, 4096], P(None, 's')
- v_w_down: float32 [2, 4096, 512], P(None, 's')
Outputs:
- output 1: bfloat16 [2, 512, 4096], P('rep', 's')
- output 2: bfloat16 [2, 512, 4096], P('rep', 's')
- output 3: bfloat16 [2, 4096, 512], P('rep', 's')
- output 4: float32 [2, 512, 4096], P('rep', 's')
- output 5: float32 [2, 512, 4096], P('rep', 's')
- output 6: float32 [2, 4096, 512], P('rep', 's')
- output 7: float32 [2, 512, 4096], P('rep', 's')
- output 8: float32 [2, 512, 4096], P('rep', 's')
- output 9: float32 [2, 4096, 512], P('rep', 's')
All inputs are finite; a program needn't handle non-finite values.
Results may differ from a plain program's by a relative error of at most 0.022.
Values are sent between devices in bfloat16 or wider.
A program may use at most 2 GiB of HBM per device.

v0:
```python
import jax
import jax.numpy as jnp
from jax import lax
from jax.sharding import PartitionSpec as P

NAMES = ("w_gate", "w_up", "w_down")


def matmul(a, w):
    return jnp.dot(a, w, preferred_element_type=jnp.float32).astype(jnp.bfloat16)


def normed(h):
    wide = h.astype(jnp.float32)
    scale = lax.rsqrt(jnp.mean(wide**2, -1, keepdims=True) + 1e-6)
    return (wide * scale).astype(jnp.bfloat16)


def layer(h, w):
    a = normed(h)
    gate = jnp.dot(a, w["w_gate"], preferred_element_type=jnp.float32)
    up = jnp.dot(a, w["w_up"], preferred_element_type=jnp.float32)
    return h + matmul((jax.nn.silu(gate) * up).astype(jnp.bfloat16), w["w_down"])


def adamw(w, m, v, g):
    m = 0.9 * m + 0.1 * g
    v = 0.95 * v + 0.05 * g * g
    step = m * lax.rsqrt(v + 1e-8) + 0.1 * w
    return (w - 0.02 * step).astype(jnp.bfloat16), m, v


def solution(mesh):
    def fetched(weights, number):
        return {name: lax.all_gather(w[number], "s", axis=0, tiled=True) for name, w in zip(NAMES, weights, strict=True)}

    def summed(term):
        return lax.psum(lax.psum_scatter(term, "s", scatter_dimension=0, tiled=True), "r")

    def step(x, dy, *arrays):
        weights, m, v = (arrays[i : i + 3] for i in (0, 3, 6))
        layers = weights[0].shape[0]
        h, kept = x[0], []
        for number in range(layers):
            kept.append(h)
            h = layer(h, fetched(weights, number))
        by_h, mine = dy[0], [None] * layers
        for number in reversed(range(layers)):
            _, back = jax.vjp(lambda w, h: layer(h, w), fetched(weights, number), kept[number])
            by_w, by_h = back(by_h)
            mine[number] = [summed(by_w[name]) for name in NAMES]
        gradients = [jnp.stack([mine[number][i] for number in range(layers)]).astype(jnp.float32) for i in range(3)]
        new = [adamw(w.astype(jnp.float32), m, v, g) for w, m, v, g in zip(weights, m, v, gradients, strict=True)]
        return tuple(one[which] for which in range(3) for one in new)

    states, cut = P(("rep", "r", "s"), None, None), P(None, "s", None)
    return jax.shard_map(
        step,
        mesh=mesh,
        in_specs=(states, states) + (cut,) * 9,
        out_specs=(P("rep", "s", None),) * 9,
        check_vma=False,
    )
```

profile of v0, /device:TPU:0, one launch (start us, length us, event | category | flops | bytes accessed | tf_op | source)
XLA Modules:
  0.0 891.4 jit_solution(16165334408607255031)
XLA Ops:
  7.2 0.0 all-gather.13.cloned.1.call-start
  7.2 2.3 fusion.85
  9.6 0.0 all-gather.13.cloned.1.call-update
  9.6 0.0 all-gather.15.cloned.1.call-start
  9.6 2.3 fusion.84
  11.9 0.0 all-gather.15.cloned.1.call-update
  11.9 0.0 all-gather.17.cloned.1.call-start
  12.0 1.0 fusion.83
  13.0 0.0 all-gather.17.cloned.1.call-update
  13.1 0.0 all-gather.21.cloned.1.call-start
  13.1 0.5 all-gather.21.cloned.1.call-update
  13.6 0.0 all-gather.23.cloned.1.call-start
  13.7 0.5 all-gather.23.cloned.1.call-update
  14.2 0.0 all-gather.19.cloned.1.call-start
  14.3 0.5 all-gather.19.cloned.1.call-update
  14.8 0.0 reduce-scatter.15.cloned.1.call-start
  14.8 6.3 copy.20
  21.2 3.1 fusion.16
  24.3 6.4 copy.21
  30.7 18.9 %all-gather.13.cloned.1.call-done = bf16[1,512,4096]{2,1,0:T(8,128)(2,1)} async-done(((bf16[1,64,4096]{2,1,0:T(8,128)(2,1)}), bf16[1,512,4096]{2,1,0:T(8,128)(2,1)}) %all-gather.13.cloned.1.call-update) | async-done | bytes 4194320 | tf_op jit(solution)/shard_map/all_gather | solution.py:35
  49.5 30.2 %fusion.46 = f32[4096,4096]{1,0:T(8,128)} fusion(bf16[1,512,4096]{2,1,0:T(8,128)(2,1)} %all-gather.13.cloned.1.call-done, bf16[1,4096,512]{1,2,0:T(8,128)(2,1)} %copy.20, f32[4096]{0:T(1024)S(1)} %add_rsqrt_fusion), kind=kOutput, calls=%fused_computation.65 | convolution fusion | flops 17186160640 | bytes 75513856 | tf_op jit(solution)/shard_map/dot_general | solution.py:21
  79.7 8.6 all-gather.15.cloned.1.call-done
  88.3 59.8 %multiply_convert_fusion.1 = (bf16[4096,4096]{1,0:T(8,128)(2,1)}, f32[4096,4096]{1,0:T(8,128)}) fusion(f32[4096,4096]{1,0:T(8,128)} %fusion.46, bf16[1,512,4096]{2,1,0:T(8,128)(2,1)} %all-gather.15.cloned.1.call-done, bf16[1,4096,512]{1,2,0:T(8,128)(2,1)} %copy.20, f32[4096]{0:T(1024)S(1)} %add_rsqrt_fusion), kind=kOutput, calls=%fused_computation.17 | convolution fusion | flops 17286823936 | bytes 176177152 | tf_op jit(solution)/shard_map/dot_general | solution.py:22
  148.1 24.6 %fusion.20 = (f32[4096]{0:T(1024)S(1)}, bf16[4096,512]{0,1:T(8,128)(2,1)}) fusion(bf16[4096,4096]{1,0:T(8,128)(2,1)} %get-tuple-element.30, bf16[1,4096,512]{2,1,0:T(8,128)(2,1)} %all-gather.17.cloned.1.call-done, bf16[1,4096,512]{1,2,0:T(8,128)(2,1)} %copy.20), kind=kOutput, calls=%fused_computation.37 | convolution fusion | flops 17190350848 | bytes 46153728 | tf_op jit(solution)/shard_map/dot_general | solution.py:10
  172.7 0.0 all-gather.21.cloned.1.call-done
  172.7 24.9 %convolution_convert_fusion.1 = bf16[4096,4096]{1,0:T(8,128)(2,1)} fusion(bf16[1,4096,512]{2,1,0:T(8,128)(2,1)} %param.12, bf16[1,4096,512]{2,1,0:T(8,128)(2,1)} %all-gather.21.cloned.1.call-done), kind=kOutput, calls=%fused_computation.25 | convolution fusion | flops 17196646400 | bytes 41943040 | tf_op jit(solution)/shard_map/transpose(jvp())/dot_general | solution.py:10
  197.6 6.8 all-gather.23.cloned.1.call-done
  204.4 30.4 %fusion.35 = f32[4096,4096]{1,0:T(8,128)} fusion(bf16[1,512,4096]{2,1,0:T(8,128)(2,1)} %all-gather.23.cloned.1.call-done, bf16[4096,512]{0,1:T(8,128)(2,1)} %get-tuple-element.33, f32[4096]{0:T(1024)S(1)} %fusion.71), kind=kOutput, calls=%fused_computation.54 | convolution fusion | flops 17186160640 | bytes 75513856 | tf_op jit(solution)/shard_map/jvp()/dot_general | solution.py:22
  234.8 8.3 all-gather.19.cloned.1.call-done
  243.1 78.8 %fusion.2 = (bf16[4096,4096]{1,0:T(8,128)(2,1)}, f32[4096,4096]{1,0:T(8,128)}) fusion(f32[4096,4096]{1,0:T(8,128)} %fusion.35, bf16[4096,4096]{1,0:T(8,128)(2,1)} %convolution_convert_fusion.1, bf16[1,512,4096]{2,1,0:T(8,128)(2,1)} %all-gather.19.cloned.1.call-done, bf16[4096,512]{0,1:T(8,128)(2,1)} %get-tuple-element.33, f32[4096]{0:T(1024)S(1)} %fusion.71), kind=kOutput, calls=%fused_computation.8 | convolution fusion | flops 17387487232 | bytes 209731584 | tf_op jit(solution)/shard_map/jvp()/dot_general | solution.py:21
  321.9 39.3 %fusion.25 = bf16[4096,512]{0,1:T(8,128)(2,1)} fusion(bf16[4096,4096]{1,0:T(8,128)(2,1)} %convolution_convert_fusion.1, bf16[1,512,4096]{2,1,0:T(8,128)(2,1)} %all-gather.23.cloned.1.call-done, f32[4096,4096]{1,0:T(8,128)} %get-tuple-element.35), kind=kOutput, calls=%fused_computation.45 | convolution fusion | flops 17282629632 | bytes 109051904 | tf_op jit(solution)/shard_map/transpose(jvp())/dot_general | solution.py:22
  361.2 33.1 %fusion.22 = (f32[4096]{0:T(1024)S(1)}, bf16[4096,512]{0,1:T(8,128)(2,1)}) fusion(bf16[4096,512]{0,1:T(8,128)(2,1)} %get-tuple-element.33, bf16[4096,512]{0,1:T(8,128)(2,1)} %fusion.25, bf16[4096,4096]{1,0:T(8,128)(2,1)} %get-tuple-element.34, bf16[1,512,4096]{2,1,0:T(8,128)(2,1)} %all-gather.19.cloned.1.call-done), kind=kOutput, calls=%fused_computation.39 | convolution fusion | flops 17190350848 | bytes 50348032 | tf_op jit(solution)/shard_map/transpose(jvp())/dot_general | solution.py:21
  394.4 6.4 fusion.32
  400.8 1.9 copy-done.3
  402.7 24.0 %convolution_convert_fusion.2 = bf16[4096,512]{1,0:T(8,128)(2,1)} fusion(bf16[4096,4096]{1,0:T(8,128)(2,1)} %get-tuple-element.30, bf16[4096,512]{0,1:T(8,128)(2,1)S(1)} %fusion.32), kind=kOutput, calls=%fused_computation.42 | convolution fusion | flops 17181966336 | bytes 41943040 | tf_op jit(solution)/shard_map/transpose(jvp())/dot_general | solution.py:10
  426.8 0.0 reduce-scatter.15.cloned.1.call-update
  426.8 0.0 reduce-scatter.17.cloned.1.call-start
  426.8 45.4 %fusion.23 = bf16[4096,512]{1,0:T(8,128)(2,1)} fusion(f32[4096,4096]{1,0:T(8,128)} %fusion.35, bf16[1,4096,512]{2,1,0:T(8,128)(2,1)} %param.12, f32[4096,4096]{1,0:T(8,128)} %get-tuple-element.35), kind=kOutput, calls=%fused_computation.40 | convolution fusion | flops 17282629632 | bytes 142606336 | tf_op jit(solution)/shard_map/transpose(jvp())/dot_general | solution.py:10
  472.2 0.0 reduce-scatter.17.cloned.1.call-update
  472.2 0.0 reduce-scatter.11.cloned.1.call-start
  472.3 24.6 %convolution_convert_fusion = bf16[4096,4096]{1,0:T(8,128)(2,1)} fusion(bf16[4096,512]{0,1:T(8,128)(2,1)} %copy-done.3, bf16[1,4096,512]{2,1,0:T(8,128)(2,1)} %all-gather.17.cloned.1.call-done), kind=kOutput, calls=%fused_computation.24 | convolution fusion | flops 17196646400 | bytes 41943040 | tf_op jit(solution)/shard_map/transpose(jvp())/dot_general | solution.py:10
  496.9 37.6 %fusion.29 = bf16[512,4096]{1,0:T(8,128)(2,1)} fusion(bf16[4096,4096]{1,0:T(8,128)(2,1)} %convolution_convert_fusion, f32[4096,4096]{1,0:T(8,128)} %fusion.46, bf16[1,4096,512]{1,2,0:T(8,128)(2,1)S(1)} %copy-done, f32[4096]{0:T(1024)S(1)} %copy-done.20), kind=kOutput, calls=%fused_computation.48 | convolution fusion | flops 17288921088 | bytes 109068288 | tf_op jit(solution)/shard_map/transpose(jvp())/dot_general | solution.py:22
  534.6 0.0 reduce-scatter.13.cloned.1.call-start
  534.6 0.6 copy-done.17
  535.3 39.4 %fusion.24 = bf16[512,4096]{1,0:T(8,128)(2,1)} fusion(bf16[4096,4096]{1,0:T(8,128)(2,1)} %convolution_convert_fusion.1, bf16[4096,512]{0,1:T(8,128)(2,1)} %get-tuple-element.33, f32[4096]{0:T(1024)S(1)} %copy-done.17, f32[4096,4096]{1,0:T(8,128)} %get-tuple-element.35), kind=kOutput, calls=%fused_computation.41 | convolution fusion | flops 17288921088 | bytes 109068288 | tf_op jit(solution)/shard_map/transpose(jvp())/dot_general | solution.py:22
  574.6 0.0 reduce-scatter.7.cloned.1.call-start
  574.7 59.3 %fusion.26 = bf16[512,4096]{1,0:T(8,128)(2,1)} fusion(f32[4096,4096]{1,0:T(8,128)} %fusion.46, f32[4096,4096]{1,0:T(8,128)} %get-tuple-element.31, bf16[4096,4096]{1,0:T(8,128)(2,1)} %convolution_convert_fusion, bf16[1,4096,512]{1,2,0:T(8,128)(2,1)} %copy.20, f32[4096]{0:T(1024)S(1)} %copy-done.20), kind=kOutput, calls=%fused_computation.47 | convolution fusion | flops 17372807168 | bytes 176177152 | tf_op jit(solution)/shard_map/transpose(jvp())/dot_general | solution.py:21
  634.0 0.0 reduce-scatter.9.cloned.1.call-start
  634.1 0.6 copy-done.18
  634.7 23.7 %convolution_convert_fusion.5 = bf16[512,4096]{1,0:T(8,128)(2,1)} fusion(bf16[4096,4096]{1,0:T(8,128)(2,1)} %get-tuple-element.34, bf16[4096,512]{0,1:T(8,128)(2,1)} %get-tuple-element.33, f32[4096]{0:T(1024)S(1)} %copy-done.18), kind=kOutput, calls=%fused_computation.46 | convolution fusion | flops 17186160640 | bytes 41959424 | tf_op jit(solution)/shard_map/transpose(jvp())/dot_general | solution.py:21
  658.4 0.0 all-reduce.3.cloned.1.call-start
  658.5 0.0 reduce-scatter.15.cloned.1.call-done
  658.5 0.0 reduce-scatter.17.cloned.1.call-done
  658.5 0.0 reduce-scatter.11.cloned.1.call-done
  658.5 0.0 reduce-scatter.13.cloned.1.call-done
  658.6 35.8 %reduce-scatter.7.cloned.1.call-done = bf16[64,4096]{1,0:T(8,128)(2,1)} async-done(((bf16[512,4096]{1,0:T(8,128)(2,1)}), bf16[64,4096]{1,0:T(8,128)(2,1)}) %reduce-scatter.7.cloned.1.call-update) | async-done | bytes 524304 | tf_op jit(solution)/shard_map/reduce_scatter | solution.py:38
  694.3 54.0 %reduce-scatter.9.cloned.1.call-done = bf16[64,4096]{1,0:T(8,128)(2,1)} async-done(((bf16[512,4096]{1,0:T(8,128)(2,1)}), bf16[64,4096]{1,0:T(8,128)(2,1)}) %reduce-scatter.9.cloned.1.call-update) | async-done | bytes 524304 | tf_op jit(solution)/shard_map/reduce_scatter | solution.py:38
  748.4 122.9 %all-reduce.3.cloned.1.call-done = (bf16[1,64,4096]{2,1,0:T(8,128)(2,1)}, bf16[1,64,4096]{2,1,0:T(8,128)(2,1)}, bf16[1,64,4096]{2,1,0:T(8,128)(2,1)}, bf16[1,64,...) async-done(((bf16[1,64,4096]{2,1,0:T(8,128)(2,1)}, bf16[1,64,4096]{2,1,0:T(8,128)(2,1)}, bf16[1,64,4096]{2,1,0:T(8,128)(2,1)}, ...) | async-done | bytes 3145744 | tf_op jit(solution)/shard_map/psum | solution.py:38
  871.4 5.3 fusion.66
  876.6 0.8 copy-done.9
  877.4 0.7 copy-done.10
  878.2 0.0 copy-done.11
  878.2 0.2 copy-done.12
  878.4 6.1 fusion.58
  (44 shorter events, 0.2 us)
Async XLA Ops:
  7.2 4.8 copy-start.4
  7.2 42.4 %all-gather.13.cloned.1.call-start = ((), (), s32[]{:S(2)}) async-start(), calls=%async_computation.12 | async-start | bytes 4718592 | tf_op jit(solution)/shard_map/all_gather | solution.py:35
  9.6 78.7 %all-gather.15.cloned.1.call-start = ((), (), s32[]{:S(2)}) async-start(), calls=%async_computation.13 | async-start | bytes 4718592 | tf_op jit(solution)/shard_map/all_gather | solution.py:35
  11.9 136.2 %all-gather.17.cloned.1.call-start = ((), (), s32[]{:S(2)}) async-start(), calls=%async_computation.14 | async-start | bytes 4718592 | tf_op jit(solution)/shard_map/all_gather | solution.py:35
  13.1 159.7 %all-gather.21.cloned.1.call-start = ((), (), s32[]{:S(2)}) async-start(), calls=%async_computation.16 | async-start | bytes 4718592 | tf_op jit(solution)/shard_map/all_gather | solution.py:35
  13.6 190.8 %all-gather.23.cloned.1.call-start = ((), (), s32[]{:S(2)}) async-start(), calls=%async_computation.17 | async-start | bytes 4718592 | tf_op jit(solution)/shard_map/all_gather | solution.py:35
  14.2 228.9 %all-gather.19.cloned.1.call-start = ((), (), s32[]{:S(2)}) async-start(), calls=%async_computation.15 | async-start | bytes 4718592 | tf_op jit(solution)/shard_map/all_gather | solution.py:35
  14.8 643.7 %reduce-scatter.15.cloned.1.call-start = ((), (), s32[]{:S(2)}) async-start(), calls=%async_computation.10 | async-start | bytes 4718592 | tf_op jit(solution)/shard_map/reduce_scatter | solution.py:38
  24.3 64.1 %copy-start.19 = (f32[4096]{0:T(1024)}, f32[4096]{0:T(1024)S(1)}, u32[]{:S(2)}) copy-start(f32[4096]{0:T(1024)S(1)} %add_rsqrt_fusion) | copy-start | bytes 49156
  172.7 24.9 %copy-start.13 = (f32[4096]{0:T(1024)}, f32[4096]{0:T(1024)S(1)}, u32[]{:S(2)}) copy-start(f32[4096]{0:T(1024)S(1)} %get-tuple-element.32) | copy-start | bytes 49156
  172.7 70.4 %copy-start.15 = (f32[4096]{0:T(1024)}, f32[4096]{0:T(1024)S(1)}, u32[]{:S(2)}) copy-start(f32[4096]{0:T(1024)S(1)} %fusion.71) | copy-start | bytes 49156
  361.2 33.1 %copy-start.14 = (f32[4096]{0:T(1024)S(1)}, f32[4096]{0:T(1024)}, u32[]{:S(2)}) copy-start(f32[4096]{0:T(1024)} %copy-done.13) | copy-start | bytes 49156
  361.2 33.2 %copy-start.16 = (f32[4096]{0:T(1024)S(1)}, f32[4096]{0:T(1024)}, u32[]{:S(2)}) copy-start(f32[4096]{0:T(1024)} %copy-done.15) | copy-start | bytes 49156
  400.8 2.0 copy-start.3
  426.8 231.7 %reduce-scatter.17.cloned.1.call-start = ((), (), s32[]{:S(2)}) async-start(), calls=%async_computation.11 | async-start | bytes 4718592 | tf_op jit(solution)/shard_map/reduce_scatter | solution.py:38
  472.2 24.7 %copy-start.20 = (f32[4096]{0:T(1024)S(1)}, f32[4096]{0:T(1024)}, u32[]{:S(2)}) copy-start(f32[4096]{0:T(1024)} %copy-done.19) | copy-start | bytes 49156
  472.2 186.3 %reduce-scatter.11.cloned.1.call-start = ((), (), s32[]{:S(2)}) async-start(), calls=%async_computation.8 | async-start | bytes 4718592 | tf_op jit(solution)/shard_map/reduce_scatter | solution.py:38
  472.3 24.6 %copy-start = (bf16[1,4096,512]{1,2,0:T(8,128)(2,1)S(1)}, bf16[1,4096,512]{1,2,0:T(8,128)(2,1)}, u32[]{:S(2)}) copy-start(bf16[1,4096,512]{1,2,0:T(8,128)(2,1)} %copy.20) | copy-start | bytes 12582916
  534.6 0.7 copy-start.17
  534.6 124.0 %reduce-scatter.13.cloned.1.call-start = ((), (), s32[]{:S(2)}) async-start(), calls=%async_computation.9 | async-start | bytes 4718592 | tf_op jit(solution)/shard_map/reduce_scatter | solution.py:38
  574.6 119.7 %reduce-scatter.7.cloned.1.call-start = ((), (), s32[]{:S(2)}) async-start(), calls=%async_computation.6 | async-start | bytes 4718592 | tf_op jit(solution)/shard_map/reduce_scatter | solution.py:38
  634.0 0.7 copy-start.18
  634.0 114.4 %reduce-scatter.9.cloned.1.call-start = ((), (), s32[]{:S(2)}) async-start(), calls=%async_computation.7 | async-start | bytes 4718592 | tf_op jit(solution)/shard_map/reduce_scatter | solution.py:38
  658.4 212.9 %copy-start.5 = (bf16[2,512,512]{2,1,0:T(8,128)(2,1)S(1)}, bf16[2,512,512]{2,1,0:T(8,128)(2,1)}, u32[]{:S(2)}) copy-start(bf16[2,512,512]{2,1,0:T(8,128)(2,1)} %param.15) | copy-start | bytes 3145732
  658.4 212.9 %copy-start.6 = (f32[2,512,512]{2,1,0:T(8,128)S(1)}, f32[2,512,512]{2,1,0:T(8,128)}, u32[]{:S(2)}) copy-start(f32[2,512,512]{2,1,0:T(8,128)} %param.21) | copy-start | bytes 6291460
  658.4 212.9 %all-reduce.3.cloned.1.call-start = ((), (), s32[]{:S(2)}) async-start(), calls=%async_computation.18 | async-start | bytes 6291456 | tf_op jit(solution)/shard_map/psum | solution.py:38
  871.3 5.3 copy-start.1
  871.3 5.3 copy-start.2
  871.3 5.3 copy-start.7
  871.3 5.3 copy-start.8
  871.3 6.1 copy-start.9
  871.3 6.9 copy-start.10
  871.4 6.9 copy-start.11
  871.4 7.0 copy-start.12
Sparse Core Ops, SparseCore 0:
  10.5 39.0 all-gather.12
  52.0 36.2 all-gather.14
  90.8 36.2 all-gather.16
  129.5 36.2 all-gather.20
  168.1 36.2 all-gather.22
  206.8 36.2 all-gather.18
  426.9 50.7 reduce-scatter.14
  481.1 50.7 reduce-scatter.16
  535.2 50.7 reduce-scatter.10
  589.3 50.7 reduce-scatter.12
  643.5 50.7 reduce-scatter.6
  697.5 50.7 reduce-scatter.8
  751.2 120.0 all-reduce.2
where the time goes:
time: 900 us; the launch traced here: 891 us
  matrix products  575 us (64%)
  waiting for transfers between devices  257 us (29%)
  local copies, waits for them, and re-layouts  23.4 us (3%)
  other arithmetic  20.8 us (2%)
  between operations  14.6 us (2%)
    dot_general x5, matrix products, layer(): gate = jnp.dot(a, w['w_gate'], preferred_element_type=jnp.float32)  225 us
    dot_general x5, matrix products, layer(): up = jnp.dot(a, w['w_up'], preferred_element_type=jnp.float32)  206 us
    dot_general x5, matrix products, matmul(): jnp.dot(a, w, preferred_element_type=jnp.float32).astype(jnp.bfloat16)  143 us
    psum x1, waiting for transfers between devices, summed(): lax.psum(lax.psum_scatter(term, 's', scatter_dimension=0, tiled=True), 'r')  123 us
    reduce_scatter x6, waiting for transfers between devices, summed(): lax.psum_scatter(term, 's', scatter_dimension=0, tiled=True)  89.9 us
    all_gather x6, waiting for transfers between devices, fetched(): lax.all_gather(w[number], 's', axis=0, tiled=True)  42.6 us
  transfers between devices with their start and end apart: 13, of which 7 were waited for; matrix products, arithmetic and copies ran while one was open for 47% of the time, Pallas kernels for 0%

commit v1 on v0

v1 whole, which is shorter than its diff:
```python
import functools

import jax
import jax.numpy as jnp
from jax import lax
from jax.experimental import pallas as pl
from jax.experimental.pallas import tpu as pltpu
from jax.sharding import PartitionSpec as P

F32, BF16 = jnp.float32, jnp.bfloat16
MESH = pl.DeviceIdType.MESH
CHUNK = 512
AHEAD = 4


def adamw(w, m, v, g):
    m = 0.9 * m + 0.1 * g
    v = 0.95 * v + 0.05 * g * g
    step = m * lax.rsqrt(v + 1e-8) + 0.1 * w
    return (w - 0.02 * step).astype(jnp.bfloat16), m, v


def dot(a, b):
    return jnp.dot(a, b, preferred_element_type=F32)


def kernel(
    x_hbm, dy_hbm, pk_hbm, full_hbm, out_hbm,
    H, DY, A, AT, DYT, acc, act, dg, du, wt, wtT, G, R0, S1, own, R1, T2, R2, T3, R3, O,
    load_sem, wt_sem, ag_send, ag_recv, fw_send, fw_recv, send0, recv0, send1, recv1, send2, recv2, send3, recv3, out_sem,
):
    tokens, d_model = H.shape
    tiles = pk_hbm.shape[0]
    half = tiles // 2
    width = act.shape[1]
    chunks = tokens // CHUNK
    s, r = lax.axis_index("s"), lax.axis_index("r")
    core, chip = s % 2, s // 2
    partner = s + 1 - 2 * core
    chips = ((chip + 2) % 4, chip + 1 - 2 * (chip % 2), (chip + 2) % 4 + 1 - 2 * (chip % 2))
    peers = [2 * c + core for c in chips]
    near = r + 1 - 2 * (r % 2)
    far = (r + 2) % 4

    barrier = pltpu.get_barrier_semaphore()
    for where in [{"s": p} for p in [partner] + peers] + [{"r": near}, {"r": far}]:
        pl.semaphore_signal(barrier, inc=1, device_id=where, device_id_type=MESH)
    pl.semaphore_wait(barrier, 6)

    def remote(src, dst, send, recv, where):
        return pltpu.make_async_remote_copy(src_ref=src, dst_ref=dst, send_sem=send, recv_sem=recv, device_id=where, device_id_type=MESH)

    def shard(tile, n):
        where = (peers + [partner])[n]
        return remote(pk_hbm.at[tile], full_hbm.at[tile, chip, core], ag_send.at[tile, n], ag_recv.at[tile, n], {"s": where})

    def passed(tile, n):
        ref = full_hbm.at[tile, chips[n], core]
        return remote(ref, ref, fw_send.at[tile, n], fw_recv.at[tile, n], {"s": partner})

    def send_shard(tile):
        for n in range(4):
            shard(tile, n).start()

    def pass_on(tile):
        for n in range(3):
            shard(tile, n).wait_recv()
            passed(tile, n).start()

    def whole(tile):
        shard(tile, 3).wait_recv()
        for n in range(3):
            passed(tile, n).wait_recv()

    def load(tile, slot):
        pltpu.make_async_copy(pk_hbm.at[tile], wt.at[slot, chip, core], wt_sem.at[slot]).start()
        for n in range(1, 8):
            d = (s + n) % 8
            pltpu.make_async_copy(full_hbm.at[tile, d // 2, d % 2], wt.at[slot, d // 2, d % 2], wt_sem.at[slot]).start()

    def loaded(slot):
        pltpu.make_async_copy(full_hbm.at[0], wt.at[slot], wt_sem.at[slot]).wait()

    def weight(slot, which):
        return wt[slot, :, :, which].reshape(width, d_model)

    def rows(t):
        return pl.ds(pl.multiple_of(t * CHUNK, CHUNK), CHUNK)

    def each_chunk(body):
        lax.fori_loop(0, chunks, lambda t, _: (body(rows(t)), None)[1], None)

    def scale_of(wide):
        return lax.rsqrt(jnp.mean(wide * wide, -1, keepdims=True) + 1e-6)

    for tile in range(AHEAD):
        send_shard(tile)
    get_x = pltpu.make_async_copy(x_hbm, H, load_sem.at[0])
    get_dy = pltpu.make_async_copy(dy_hbm, DY, load_sem.at[1])
    get_x.start()
    get_dy.start()
    get_x.wait()

    def prepare_forward(at):
        wide = H[at].astype(F32)
        A[at] = (wide * scale_of(wide)).astype(BF16)
        acc[at] = jnp.zeros((CHUNK, d_model), F32)

    each_chunk(prepare_forward)
    pass_on(0)
    whole(0)
    load(0, 0)

    def forward(k, _):
        slot = k % 2
        send_shard(k + AHEAD)
        pass_on(k + 1)
        loaded(slot)

        def body(at):
            a = A[at]
            gate = dot(a, weight(slot, 0))
            up = dot(a, weight(slot, 1))
            sig = 0.5 * jnp.tanh(0.5 * gate) + 0.5
            acc[at] += dot((gate * sig * up).astype(BF16), weight(slot, 2))

        each_chunk(body)
        whole(k + 1)
        load(k + 1, 1 - slot)

    lax.fori_loop(0, half, forward, None)
    get_dy.wait()

    def prepare_last(at):
        h = (H[at].astype(F32) + acc[at].astype(BF16).astype(F32)).astype(BF16)
        H[at] = h
        wide = h.astype(F32)
        a = (wide * scale_of(wide)).astype(BF16)
        A[at] = a
        AT[:, at] = a.T
        DYT[:, at] = DY[at].T
        acc[at] = jnp.zeros((CHUNK, d_model), F32)

    each_chunk(prepare_last)

    def prepare_first(at):
        wide = H[at].astype(F32)
        scale = scale_of(wide)
        ct = acc[at].astype(BF16).astype(F32)
        by = ct * scale - wide * (jnp.sum(ct * wide, -1, keepdims=True) * (scale * scale * scale) * (1.0 / d_model))
        by = (DY[at].astype(F32) + by.astype(BF16).astype(F32)).astype(BF16)
        DY[at] = by
        DYT[:, at] = by.T

    def prepare_first_a(at):
        wide = H[at].astype(F32)
        a = (wide * scale_of(wide)).astype(BF16)
        A[at] = a
        AT[:, at] = a.T

    def stage0(i):
        slot = i % 2
        return remote(G.at[slot, :, 1 - core], R0.at[slot], send0, recv0.at[slot], {"s": partner})

    def stage1(i, n):
        slot = i % 2
        return remote(S1.at[chips[n]], R1.at[slot, n], send1.at[n], recv1.at[slot, n], {"s": peers[n]})

    def stage2(i):
        return remote(T2, R2.at[i % 2], send2, recv2.at[i % 2], {"r": near})

    def stage3(i):
        return remote(T3, R3.at[i % 2], send3, recv3.at[i % 2], {"r": far})

    def put(i):
        return pltpu.make_async_copy(O, out_hbm.at[i], out_sem)

    def when(i, lo, hi):
        return pl.when(jnp.logical_and(i >= lo, i < hi))

    def sums(q):
        def done(i, copies):
            @when(i, 1, tiles + 1)
            def _():
                for copy in copies(i - 1):
                    copy()

        i4 = q - 4
        done(i4, lambda i: [put(i).wait])

        @when(i4, 0, tiles)
        def _():
            stage3(i4).wait_recv()
            O[...] = (T3[...].astype(F32) + R3[i4 % 2].astype(F32)).astype(BF16)
            put(i4).start()

        i3 = q - 3
        done(i3, lambda i: [stage3(i).wait_send])

        @when(i3, 0, tiles)
        def _():
            stage2(i3).wait_recv()
            T3[...] = (T2[...].astype(F32) + R2[i3 % 2].astype(F32)).astype(BF16)
            stage3(i3).start()

        i2 = q - 2
        done(i2, lambda i: [stage2(i).wait_send])

        @when(i2, 0, tiles)
        def _():
            for n in range(3):
                stage1(i2, n).wait_recv()
            slot = i2 % 2
            T2[...] = (own[...] + R1[slot, 0].astype(F32) + R1[slot, 1].astype(F32) + R1[slot, 2].astype(F32)).astype(BF16)
            stage2(i2).start()

        i1 = q - 1
        done(i1, lambda i: [stage1(i, n).wait_send for n in range(3)])

        @when(i1, 0, tiles)
        def _():
            stage0(i1).wait()
            slot = i1 % 2
            own[...] = G[slot, chip, core].astype(F32) + R0[slot, chip].astype(F32)
            for c in range(4):
                S1[c] = (G[slot, c, core].astype(F32) + R0[slot, c].astype(F32)).astype(BF16)
            for n in range(3):
                stage1(i1, n).start()

        @when(q, 0, tiles)
        def _():
            stage0(q).start()

    def backward(q, _):
        slot = q % 2

        @pl.when(q == half)
        def _():
            each_chunk(prepare_first)
            again = pltpu.make_async_copy(x_hbm, H, load_sem.at[0])
            again.start()
            again.wait()
            each_chunk(prepare_first_a)

        @pl.when(q < half - AHEAD)
        def _():
            send_shard(q + half + AHEAD)

        @pl.when(q < half - 1)
        def _():
            pass_on(q + half + 1)

        @pl.when(q < tiles)
        def _():
            loaded(slot)
            for which in range(3):
                wtT[which] = weight(slot, which).T

            def body(at):
                a = A[at]
                gate = dot(a, weight(slot, 0))
                up = dot(a, weight(slot, 1))
                by = dot(DY[at], wtT[2]).astype(BF16).astype(F32)
                sig = 0.5 * jnp.tanh(0.5 * gate) + 0.5
                silu = gate * sig
                act[at] = (silu * up).astype(BF16)
                du[at] = (by * silu).astype(BF16)
                dg[at] = (by * up * (sig + silu * (1.0 - sig))).astype(BF16)

            each_chunk(body)

            @pl.when(q < half)
            def _():
                def body(at):
                    acc[at] += dot(dg[at], wtT[0]) + dot(du[at], wtT[1])

                each_chunk(body)

            def keep(which, value):
                G[slot, :, :, which] = value.reshape(4, 2, d_model // 8, width)

            keep(0, dot(AT[...], dg[...]).astype(BF16))
            keep(1, dot(AT[...], du[...]).astype(BF16))
            keep(2, dot(DYT[...], act[...]).astype(BF16).T)

        sums(q)

        @pl.when(q < half - 1)
        def _():
            whole(q + half + 1)
            load(q + half + 1, 1 - slot)

        @pl.when(jnp.logical_and(q >= half - 1, q < tiles - 1))
        def _():
            load(q - half + 1, 1 - slot)

    lax.fori_loop(0, tiles + 5, backward, None)

    def sent(tile, _):
        for n in range(4):
            shard(tile, n).wait_send()
        for n in range(3):
            passed(tile, n).wait_send()

    lax.fori_loop(0, tiles, sent, None)


def gradients_of(x, dy, packed):
    tiles, _, height, width = packed.shape
    tokens, d_model = x.shape
    piece = (3, height, width)
    vmem, sem = pltpu.VMEM, pltpu.SemaphoreType.DMA
    flops = 17 * 2 * tokens * d_model * width * tiles // 2
    _, out = pl.pallas_call(
        kernel,
        out_shape=(jax.ShapeDtypeStruct((tiles, 4, 2) + piece, BF16), jax.ShapeDtypeStruct((tiles,) + piece, BF16)),
        in_specs=[pl.BlockSpec(memory_space=pltpu.HBM)] * 3,
        out_specs=[pl.BlockSpec(memory_space=pltpu.HBM)] * 2,
        scratch_shapes=[
            vmem((tokens, d_model), BF16),
            vmem((tokens, d_model), BF16),
            vmem((tokens, d_model), BF16),
            vmem((d_model, tokens), BF16),
            vmem((d_model, tokens), BF16),
            vmem((tokens, d_model), F32),
            vmem((tokens, width), BF16),
            vmem((tokens, width), BF16),
            vmem((tokens, width), BF16),
            vmem((2, 4, 2) + piece, BF16),
            vmem((3, d_model, width), BF16),
            vmem((2, 4, 2) + piece, BF16),
            vmem((2, 4) + piece, BF16),
            vmem((4,) + piece, BF16),
            vmem(piece, F32),
            vmem((2, 3) + piece, BF16),
            vmem(piece, BF16),
            vmem((2,) + piece, BF16),
            vmem(piece, BF16),
            vmem((2,) + piece, BF16),
            vmem(piece, BF16),
            sem((2,)),
            sem((2,)),
            sem((tiles, 4)),
            sem((tiles, 4)),
            sem((tiles, 3)),
            sem((tiles, 3)),
            sem, sem((2,)),
            sem((3,)), sem((2, 3)),
            sem, sem((2,)),
            sem, sem((2,)),
            sem,
        ],
        compiler_params=pltpu.CompilerParams(collective_id=0, has_side_effects=True, vmem_limit_bytes=67043328),
        cost_estimate=pl.CostEstimate(flops=flops, bytes_accessed=64 << 20, transcendentals=0),
        name="step",
    )(x, dy, packed)
    return out


def solution(mesh):
    def pack(gate, up, down):
        rows, hidden = gate.shape

        def columns(w):
            return w.reshape(rows, 8, 8, hidden // 64).transpose(2, 0, 1, 3).reshape(8, rows, hidden // 8)

        return jnp.stack([columns(gate), columns(up), down.reshape(8, -1, down.shape[1])], 1)

    def unpack(tiles):
        def columns(t):
            j, rows, width = t.shape
            return t.reshape(j, rows, 8, width // 8).transpose(1, 2, 0, 3).reshape(rows, j * width)

        return columns(tiles[:, 0]), columns(tiles[:, 1]), tiles[:, 2].reshape(-1, tiles.shape[3])

    def step(x, dy, *arrays):
        weights, m, v = (arrays[i : i + 3] for i in (0, 3, 6))
        layers = weights[0].shape[0]
        packed = jnp.concatenate([pack(*(w[number] for w in weights)) for number in range(layers)])
        out = gradients_of(x[0], dy[0], packed)
        half = out.shape[0] // 2
        mine = [unpack(out[half:]), unpack(out[:half])]
        gradients = [jnp.stack([mine[number][i] for number in range(layers)]).astype(jnp.float32) for i in range(3)]
        new = [adamw(w.astype(jnp.float32), m, v, g) for w, m, v, g in zip(weights, m, v, gradients, strict=True)]
        return tuple(one[which] for which in range(3) for one in new)

    states, cut = P(("rep", "r", "s"), None, None), P(None, "s", None)
    return jax.shard_map(
        step,
        mesh=mesh,
        in_specs=(states, states) + (cut,) * 9,
        out_specs=(P("rep", "s", None),) * 9,
        check_vma=False,
    )
```

time: 900 us -> 535 us (0.59)
  matrix products: 575 us -> 0 us
  Pallas kernels: 0 us -> 483 us
  waiting for transfers between devices: 257 us -> 0 us
  between operations: 14.6 us -> 0.93 us
  local copies, waits for them, and re-layouts: 23.4 us -> 35.2 us
    dot_general x15 -> x0, matrix products: 575 us -> none  [the longest x5 225 us: layer(): gate = jnp.dot(a, w['w_gate'], preferred_element_type=jnp.float32)]
    pallas_call x0 -> x1, Pallas kernels: none -> 483 us  [gradients_of(): pl.pallas_call(kernel, out_shape=(jax.ShapeDtypeStruct((tiles, 4, 2) + pi...]
    psum x1 -> x0, waiting for transfers between devices: 123 us -> none  [summed(): lax.psum(lax.psum_scatter(term, 's', scatter_dimension=0, tiled=True), 'r')]
    reduce_scatter x6 -> x0, waiting for transfers between devices: 89.9 us -> none  [summed(): lax.psum_scatter(term, 's', scatter_dimension=0, tiled=True)]
    all_gather x6 -> x0, waiting for transfers between devices: 42.6 us -> none  [fetched(): lax.all_gather(w[number], 's', axis=0, tiled=True)]
    another operation x0 -> x20, local copies, waits for them, and re-layouts: none -> 21.6 us  [the longest x8 6.9 us: columns(): w.reshape(rows, 8, 8, hidden // 64).transpose(2, 0, 1, 3)]
    unnamed x44 -> x30, local copies, waits for them, and re-layouts: 17.8 us -> 2.55 us
  transfers between devices with their start and end apart: 13 -> 0, of which waited for: 7 -> 0; matrix products, arithmetic and copies ran while one was open for 47% -> 0% of each run, Pallas kernels for 0% -> 0%
where the time goes in v1:
time: 535 us; the launch traced here: 534 us
  Pallas kernels  483 us (90%)
  local copies, waits for them, and re-layouts  35.2 us (7%)
  other arithmetic  14 us (3%)
    pallas_call x1, Pallas kernels, gradients_of(): pl.pallas_call(kernel, out_shape=(jax.ShapeDtypeStruct((tiles, 4, 2) + pi...  483 us
    convert_element_type x2, other arithmetic, adamw(): return ((w - 0.02 * step).astype(jnp.bfloat16), m, v)  12.2 us

profile of v1, /device:TPU:0, one launch (start us, length us, event | category | flops | bytes accessed | tf_op | source)
XLA Modules:
  0.0 533.6 jit_solution(16983093381061941004)
XLA Ops:
  0.6 2.1 fusion.22
  2.7 1.1 reshape_squeeze.24
  3.8 0.1 copy.35
  4.0 1.4 stack_reshape.24
  5.4 2.1 reshape_squeeze.26
  7.5 0.0 copy-start.1
  7.5 0.1 copy.33
  7.6 1.4 stack_reshape.26
  9.0 0.0 copy-done.1
  9.0 0.9 fusion.23
  9.9 1.1 reshape_squeeze.25
  11.0 0.1 copy.34
  11.2 1.4 stack_reshape.25
  12.6 2.1 reshape_squeeze.27
  14.7 0.0 copy-start.3
  14.7 0.1 copy.32
  14.8 0.0 copy-start.6
  14.8 0.0 copy-start.8
  14.8 1.4 stack_reshape.27
  16.2 0.0 copy-done.3
  16.2 0.0 copy-start.10
  16.3 0.0 copy-start.11
  16.3 0.1 fusion.24
  16.3 0.0 copy-done.6
  16.3 0.0 copy-done.8
  16.3 0.9 copy-done.10
  17.3 0.2 copy-done.11
  17.4 1.9 maximum_maximum_fusion.pk_hbm
  19.3 483.4 %step.1 = (bf16[16,4,2,3,64,512]{5,4,3,2,1,0:T(8,128)(2,1)}, bf16[16,3,64,512]{3,2,1,0:T(8,128)(2,1)}) custom-call(bf16[4096,512]{1,0:T(8,128)(2,1)} %bitcast.58, bf16[4096,512]{1,0:T(8,128)(2,1)} %bitcast.59, bf16[16,3,64,512]{3,2,1,0:T(8,128)(2,1)} %maximum_maximum_fusion.pk_hbm), custom_call_target="tpu_custom_call" | custom-call | flops 292057776128 | bytes 67108864 | tf_op jit(solution)/shard_map/step/pallas_call | solution.py:314
  502.8 3.1 fusion.21
  505.9 0.5 reshape_squeeze.31
  506.4 1.2 copy.27
  507.6 1.6 stack_reshape.31
  509.2 1.9 reshape_squeeze.30
  511.1 1.2 copy.26
  512.3 1.6 stack_reshape.30
  513.9 0.5 reshape_squeeze.29
  514.5 1.2 copy.25
  515.7 1.6 stack_reshape.29
  517.3 0.5 reshape_squeeze.28
  517.9 0.0 copy-start.4
  517.9 1.2 copy.24
  519.1 0.8 stack_reshape.28
  519.9 0.0 copy-done.4
  519.9 0.0 copy-start
  519.9 0.0 copy-start.2
  519.9 0.0 copy-start.5
  520.0 0.0 copy-start.7
  520.0 0.0 copy-start.9
  520.0 0.0 copy-start.12
  520.0 0.0 copy-start.13
  520.0 0.0 copy-start.14
  520.0 5.9 %fusion.10 = (bf16[2,512,512]{2,1,0:T(8,128)(2,1)}, f32[2,512,512]{2,1,0:T(8,128)}, f32[2,512,512]{2,1,0:T(8,128)}) fusion(bf16[2,512,512]{2,1,0:T(8,128)(2,1)S(1)} %copy-done.4, bf16[1,512,512]{2,1,0:T(8,128)(2,1)} %bitcast.55, bf16[1,512,512]{2,1,0:T(8,128)(2,1)} %bitcast.54, f32[2,512,512]{2,1,0:T(8,128)} %param.21, f32[2,512,512]{2,1,0:T(8,128)} %param.18), kind=kLoop, calls=%fused_computation.23 | loop fusion | flops 9961472 | bytes 11534336 | tf_op jit(solution)/shard_map/convert_element_type | solution.py:20
  525.9 0.0 copy-done
  525.9 0.0 copy-done.2
  525.9 0.0 copy-done.5
  525.9 0.0 copy-done.7
  525.9 0.0 copy-done.9
  525.9 0.0 copy-done.12
  525.9 0.2 copy-done.13
  526.2 1.1 copy-done.14
  527.3 6.3 %fusion.2 = (bf16[2,64,4096]{2,1,0:T(8,128)(2,1)}, f32[2,64,4096]{2,1,0:T(8,128)}, f32[2,64,4096]{2,1,0:T(8,128)}, bf16[2,64,4096]{2,1,0:T(8,128)(2,1)}, f32[2,64,4096]{2,1,0:T(8,128)}, /*index=5*/f32[2,64,4096]{2,1,0:T(8,128)}) fusion(bf16[2,64,4096]{2,1,0:T(8,128)(2,1)S(1)} %copy-done, bf16[1,64,4096]{2,1,0:T(8,128)(2,1)S(1)} %copy-done.9, ...), kind=kLoop, calls=%fused_computation.15 | loop fusion | flops 19922944 | bytes 23068672 | tf_op jit(solution)/shard_map/convert_element_type | solution.py:20
Async XLA Ops:
  7.5 1.6 copy-start.1
  14.7 1.6 copy-start.3
  14.8 1.5 copy-start.6
  14.8 1.5 copy-start.8
  16.2 1.0 copy-start.10
  16.3 1.2 copy-start.11
  517.9 2.1 copy-start.4
  519.9 6.0 %copy-start = (bf16[2,64,4096]{2,1,0:T(8,128)(2,1)S(1)}, bf16[2,64,4096]{2,1,0:T(8,128)(2,1)}, u32[]{:S(2)}) copy-start(bf16[2,64,4096]{2,1,0:T(8,128)(2,1)} %param.13) | copy-start | bytes 3145732
  519.9 6.0 %copy-start.2 = (bf16[2,64,4096]{2,1,0:T(8,128)(2,1)S(1)}, bf16[2,64,4096]{2,1,0:T(8,128)(2,1)}, u32[]{:S(2)}) copy-start(bf16[2,64,4096]{2,1,0:T(8,128)(2,1)} %param.14) | copy-start | bytes 3145732
  519.9 6.0 %copy-start.5 = (bf16[1,64,4096]{2,1,0:T(8,128)(2,1)S(1)}, bf16[1,64,4096]{2,1,0:T(8,128)(2,1)}, u32[]{:S(2)}) copy-start(bf16[1,64,4096]{2,1,0:T(8,128)(2,1)} %stack_reshape.31) | copy-start | bytes 1572868
  520.0 5.9 %copy-start.7 = (bf16[1,64,4096]{2,1,0:T(8,128)(2,1)S(1)}, bf16[1,64,4096]{2,1,0:T(8,128)(2,1)}, u32[]{:S(2)}) copy-start(bf16[1,64,4096]{2,1,0:T(8,128)(2,1)} %stack_reshape.30) | copy-start | bytes 1572868
  520.0 5.9 %copy-start.9 = (bf16[1,64,4096]{2,1,0:T(8,128)(2,1)S(1)}, bf16[1,64,4096]{2,1,0:T(8,128)(2,1)}, u32[]{:S(2)}) copy-start(bf16[1,64,4096]{2,1,0:T(8,128)(2,1)} %stack_reshape.29) | copy-start | bytes 1572868
  520.0 5.9 %copy-start.12 = (f32[2,64,4096]{2,1,0:T(8,128)S(1)}, f32[2,64,4096]{2,1,0:T(8,128)}, u32[]{:S(2)}) copy-start(f32[2,64,4096]{2,1,0:T(8,128)} %param.19) | copy-start | bytes 6291460
  520.0 6.2 %copy-start.13 = (f32[2,64,4096]{2,1,0:T(8,128)S(1)}, f32[2,64,4096]{2,1,0:T(8,128)}, u32[]{:S(2)}) copy-start(f32[2,64,4096]{2,1,0:T(8,128)} %param.16) | copy-start | bytes 6291460
  520.0 7.3 %copy-start.14 = (f32[2,64,4096]{2,1,0:T(8,128)S(1)}, f32[2,64,4096]{2,1,0:T(8,128)}, u32[]{:S(2)}) copy-start(f32[2,64,4096]{2,1,0:T(8,128)} %param.20) | copy-start | bytes 6291460

commit v2 on v1

--- a/solution.py
+++ b/solution.py
@@ -26,13 +26,14 @@
 
 def kernel(
     x_hbm, dy_hbm, pk_hbm, full_hbm, out_hbm,
-    H, DY, A, AT, DYT, acc, act, dg, du, wt, wtT, G, R0, S1, own, R1, T2, R2, T3, R3, O,
+    H, DY, A, AT, DYT, acc, act0, act1, dg0, dg1, du0, du1, wt, wtT, G, R0, S1, own, R1, T2, R2, T3, R3, O,
     load_sem, wt_sem, ag_send, ag_recv, fw_send, fw_recv, send0, recv0, send1, recv1, send2, recv2, send3, recv3, out_sem,
 ):
     tokens, d_model = H.shape
     tiles = pk_hbm.shape[0]
     half = tiles // 2
-    width = act.shape[1]
+    width = act0.shape[1]
+    act, dg, du = (act0, act1), (dg0, dg1), (du0, du1)
     chunks = tokens // CHUNK
     s, r = lax.axis_index("s"), lax.axis_index("r")
     core, chip = s % 2, s // 2
@@ -88,7 +89,18 @@
         return pl.ds(pl.multiple_of(t * CHUNK, CHUNK), CHUNK)
 
     def each_chunk(body):
-        lax.fori_loop(0, chunks, lambda t, _: (body(rows(t)), None)[1], None)
+        lax.fori_loop(0, chunks, lambda t, _: (body(rows(t), column(t)), None)[1], None)
+
+    def column(t):
+        return pl.ds(pl.multiple_of(t // 2 * CHUNK + t % 2 * (tokens // 2), CHUNK), CHUNK)
+
+    def each_pair(body, between=None):
+        def pair(p, _):
+            body(p, [rows(2 * p), rows(2 * p + 1)])
+            if between is not None:
+                pl.when(p == chunks // 4)(between)
+
+        lax.fori_loop(0, chunks // 2, pair, None)
 
     def scale_of(wide):
         return lax.rsqrt(jnp.mean(wide * wide, -1, keepdims=True) + 1e-6)
@@ -101,7 +113,7 @@
     get_dy.start()
     get_x.wait()
 
-    def prepare_forward(at):
+    def prepare_forward(at, to):
         wide = H[at].astype(F32)
         A[at] = (wide * scale_of(wide)).astype(BF16)
         acc[at] = jnp.zeros((CHUNK, d_model), F32)
@@ -114,49 +126,50 @@
     def forward(k, _):
         slot = k % 2
         send_shard(k + AHEAD)
-        pass_on(k + 1)
         loaded(slot)
 
-        def body(at):
-            a = A[at]
-            gate = dot(a, weight(slot, 0))
-            up = dot(a, weight(slot, 1))
-            sig = 0.5 * jnp.tanh(0.5 * gate) + 0.5
-            acc[at] += dot((gate * sig * up).astype(BF16), weight(slot, 2))
-
-        each_chunk(body)
+        def body(p, both):
+            for at in both:
+                a = A[at]
+                gate = dot(a, weight(slot, 0))
+                up = dot(a, weight(slot, 1))
+                sig = 0.5 * jnp.tanh(0.5 * gate) + 0.5
+                acc[at] += dot((gate * sig * up).astype(BF16), weight(slot, 2))
+
+        each_pair(body, lambda: pass_on(k + 1))
         whole(k + 1)
         load(k + 1, 1 - slot)
 
     lax.fori_loop(0, half, forward, None)
+    pass_on(half + 1)
     get_dy.wait()
 
-    def prepare_last(at):
+    def prepare_last(at, to):
         h = (H[at].astype(F32) + acc[at].astype(BF16).astype(F32)).astype(BF16)
         H[at] = h
         wide = h.astype(F32)
         a = (wide * scale_of(wide)).astype(BF16)
         A[at] = a
-        AT[:, at] = a.T
-        DYT[:, at] = DY[at].T
+        AT[:, to] = a.T
+        DYT[:, to] = DY[at].T
         acc[at] = jnp.zeros((CHUNK, d_model), F32)
 
     each_chunk(prepare_last)
 
-    def prepare_first(at):
+    def prepare_first(at, to):
         wide = H[at].astype(F32)
         scale = scale_of(wide)
         ct = acc[at].astype(BF16).astype(F32)
         by = ct * scale - wide * (jnp.sum(ct * wide, -1, keepdims=True) * (scale * scale * scale) * (1.0 / d_model))
         by = (DY[at].astype(F32) + by.astype(BF16).astype(F32)).astype(BF16)
         DY[at] = by
-        DYT[:, at] = by.T
-
-    def prepare_first_a(at):
+        DYT[:, to] = by.T
+
+    def prepare_first_a(at, to):
         wide = H[at].astype(F32)
         a = (wide * scale_of(wide)).astype(BF16)
         A[at] = a
-        AT[:, at] = a.T
+        AT[:, to] = a.T
 
     def stage0(i):
         slot = i % 2
@@ -246,53 +259,62 @@
         def _():
             send_shard(q + half + AHEAD)
 
-        @pl.when(q < half - 1)
-        def _():
-            pass_on(q + half + 1)
-
         @pl.when(q < tiles)
         def _():
             loaded(slot)
             for which in range(3):
                 wtT[which] = weight(slot, which).T
 
-            def body(at):
-                a = A[at]
-                gate = dot(a, weight(slot, 0))
-                up = dot(a, weight(slot, 1))
-                by = dot(DY[at], wtT[2]).astype(BF16).astype(F32)
-                sig = 0.5 * jnp.tanh(0.5 * gate) + 0.5
-                silu = gate * sig
-                act[at] = (silu * up).astype(BF16)
-                du[at] = (by * silu).astype(BF16)
-                dg[at] = (by * up * (sig + silu * (1.0 - sig))).astype(BF16)
-
-            each_chunk(body)
+            def front(p, both):
+                for n, at in enumerate(both):
+                    a = A[at]
+                    gate = dot(a, weight(slot, 0))
+                    up = dot(a, weight(slot, 1))
+                    by = dot(DY[at], wtT[2]).astype(BF16).astype(F32)
+                    sig = 0.5 * jnp.tanh(0.5 * gate) + 0.5
+                    silu = gate * sig
+                    act[n][rows(p)] = (silu * up).astype(BF16)
+                    du[n][rows(p)] = (by * silu).astype(BF16)
+                    dg[n][rows(p)] = (by * up * (sig + silu * (1.0 - sig))).astype(BF16)
+
+            def both_ways(p, both):
+                front(p, both)
+                for n, at in enumerate(both):
+                    acc[at] += dot(dg[n][rows(p)], wtT[0]) + dot(du[n][rows(p)], wtT[1])
 
             @pl.when(q < half)
             def _():
-                def body(at):
-                    acc[at] += dot(dg[at], wtT[0]) + dot(du[at], wtT[1])
-
-                each_chunk(body)
+                each_pair(both_ways)
+
+            @pl.when(q >= half)
+            def _():
+                each_pair(front)
+
+            @pl.when(q < half - 2)
+            def _():
+                pass_on(q + half + 2)
+
+            @pl.when(q < half - 1)
+            def _():
+                whole(q + half + 1)
+                load(q + half + 1, 1 - slot)
+
+            @pl.when(jnp.logical_and(q >= half - 1, q < tiles - 1))
+            def _():
+                load(q - half + 1, 1 - slot)
+
+            def over_tokens(left, right):
+                cut = tokens // 2
+                return dot(left[:, :cut], right[0][...]) + dot(left[:, cut:], right[1][...])
 
             def keep(which, value):
                 G[slot, :, :, which] = value.reshape(4, 2, d_model // 8, width)
 
-            keep(0, dot(AT[...], dg[...]).astype(BF16))
-            keep(1, dot(AT[...], du[...]).astype(BF16))
-            keep(2, dot(DYT[...], act[...]).astype(BF16).T)
+            keep(0, over_tokens(AT, dg).astype(BF16))
+            keep(1, over_tokens(AT, du).astype(BF16))
+            keep(2, over_tokens(DYT, act).astype(BF16).T)
 
         sums(q)
-
-        @pl.when(q < half - 1)
-        def _():
-            whole(q + half + 1)
-            load(q + half + 1, 1 - slot)
-
-        @pl.when(jnp.logical_and(q >= half - 1, q < tiles - 1))
-        def _():
-            load(q - half + 1, 1 - slot)
 
     lax.fori_loop(0, tiles + 5, backward, None)
 
@@ -323,9 +345,7 @@
             vmem((d_model, tokens), BF16),
             vmem((d_model, tokens), BF16),
             vmem((tokens, d_model), F32),
-            vmem((tokens, width), BF16),
-            vmem((tokens, width), BF16),
-            vmem((tokens, width), BF16),
+            *[vmem((tokens // 2, width), BF16)] * 6,
             vmem((2, 4, 2) + piece, BF16),
             vmem((3, d_model, width), BF16),
             vmem((2, 4, 2) + piece, BF16),
@@ -357,32 +377,81 @@
     return out
 
 
+def swapped(t):
+    return pltpu.roll(t, 64, 1)
+
+
+def woven(left, right, odd):
+    low = lax.broadcasted_iota(jnp.int32, left.shape, 1) < 64
+    return jnp.where(low, swapped(left), right) if odd else jnp.where(low, left, swapped(right))
+
+
+def lanes(n):
+    return slice(128 * n, 128 * (n + 1))
+
+
+def pack_kernel(gate, up, down, out):
+    for which, ref in enumerate((gate, up)):
+        for p in range(4):
+            for e in range(4):
+                left, right = (ref[0, :, lanes(4 * d + p)].astype(F32) for d in (2 * e, 2 * e + 1))
+                for odd in range(2):
+                    out[2 * p + odd, which, :, lanes(e)] = woven(left, right, odd).astype(BF16)
+    for j in range(8):
+        out[j, 2] = down[0, j]
+
+
+def adamw_kernel(g, *refs):
+    ins, outs = refs[:9], refs[9:]
+
+    def update(which, at, gradient):
+        new = adamw(ins[which][at].astype(F32), ins[3 + which][at], ins[6 + which][at], gradient)
+        for k in range(3):
+            outs[3 * k + which][at] = new[k]
+
+    for which in range(2):
+        for p in range(4):
+            for e in range(4):
+                left, right = (g[2 * p + odd, which, :, lanes(e)].astype(F32) for odd in range(2))
+                for odd in range(2):
+                    update(which, (0, slice(None), lanes(4 * (2 * e + odd) + p)), woven(left, right, odd))
+    for j in range(8):
+        update(2, (0, j), g[j, 2].astype(F32))
+
+
 def solution(mesh):
-    def pack(gate, up, down):
-        rows, hidden = gate.shape
-
-        def columns(w):
-            return w.reshape(rows, 8, 8, hidden // 64).transpose(2, 0, 1, 3).reshape(8, rows, hidden // 8)
-
-        return jnp.stack([columns(gate), columns(up), down.reshape(8, -1, down.shape[1])], 1)
-
-    def unpack(tiles):
-        def columns(t):
-            j, rows, width = t.shape
-            return t.reshape(j, rows, 8, width // 8).transpose(1, 2, 0, 3).reshape(rows, j * width)
-
-        return columns(tiles[:, 0]), columns(tiles[:, 1]), tiles[:, 2].reshape(-1, tiles.shape[3])
-
     def step(x, dy, *arrays):
-        weights, m, v = (arrays[i : i + 3] for i in (0, 3, 6))
-        layers = weights[0].shape[0]
-        packed = jnp.concatenate([pack(*(w[number] for w in weights)) for number in range(layers)])
+        layers, height, hidden = arrays[0].shape
+        d_model = arrays[2].shape[2]
+        rows = 16
+
+        def tiled(w):
+            return w.reshape(layers, 8, height, d_model)
+
+        arrays = [tiled(w) if n % 3 == 2 else w for n, w in enumerate(arrays)]
+        wide = pl.BlockSpec((1, rows, hidden), lambda l, n: (l, n, 0))
+        tall = pl.BlockSpec((1, 8, rows, d_model), lambda l, n: (l, 0, n, 0))
+        each = [wide, wide, tall]
+        grid = (layers, height // rows)
+        tiles = (8, 3, rows, hidden // 8)
+        packed = pl.pallas_call(
+            pack_kernel,
+            out_shape=jax.ShapeDtypeStruct((8 * layers, 3, height, hidden // 8), BF16),
+            grid=grid,
+            in_specs=each,
+            out_specs=pl.BlockSpec(tiles, lambda l, n: (l, 0, n, 0)),
+            name="pack",
+        )(*arrays[:3])
         out = gradients_of(x[0], dy[0], packed)
-        half = out.shape[0] // 2
-        mine = [unpack(out[half:]), unpack(out[:half])]
-        gradients = [jnp.stack([mine[number][i] for number in range(layers)]).astype(jnp.float32) for i in range(3)]
-        new = [adamw(w.astype(jnp.float32), m, v, g) for w, m, v, g in zip(weights, m, v, gradients, strict=True)]
-        return tuple(one[which] for which in range(3) for one in new)
+        new = pl.pallas_call(
+            adamw_kernel,
+            out_shape=[jax.ShapeDtypeStruct(a.shape, a.dtype) for a in arrays],
+            grid=grid,
+            in_specs=[pl.BlockSpec(tiles, lambda l, n: (layers - 1 - l, 0, n, 0))] + each * 3,
+            out_specs=each * 3,
+            name="adamw",
+        )(out, *arrays)
+        return tuple(w.reshape(layers, 8 * height, d_model) if n % 3 == 2 else w for n, w in enumerate(new))
 
     states, cut = P(("rep", "r", "s"), None, None), P(None, "s", None)
     return jax.shard_map(

time: 535 us -> 463 us (0.87)
  local copies, waits for them, and re-layouts: 35.2 us -> 0 us
  Pallas kernels: 483 us -> 462 us
  other arithmetic: 14 us -> 0 us
    pallas_call x1, Pallas kernels: 483 us -> 440 us  [gradients_of(): pl.pallas_call(kernel, out_shape=(jax.ShapeDtypeStruct((tiles, 4, 2) + pi...]
    another operation x20 -> x0, local copies, waits for them, and re-layouts: 21.6 us -> none  [the longest x8 6.9 us: columns(): w.reshape(rows, 8, 8, hidden // 64).transpose(2, 0, 1, 3)]
    pallas_call x0 -> x2, Pallas kernels: none -> 21.5 us  [the longest x1 14.8 us: step(): pl.pallas_call(adamw_kernel, out_shape=[jax.ShapeDtypeStruct(a.shape, a.d...]
    convert_element_type x2 -> x0, other arithmetic: 12.2 us -> none  [adamw(): return ((w - 0.02 * step).astype(jnp.bfloat16), m, v)]
    slice x4 -> x0, local copies, waits for them, and re-layouts: 6.11 us -> none  [the longest x1 3.09 us: unpack(): tiles[:, 2].reshape(-1, tiles.shape[3])]
where the time goes in v2:
time: 463 us; the launch traced here: 462 us
  Pallas kernels  462 us (100%)
    pallas_call x1, Pallas kernels, gradients_of(): pl.pallas_call(kernel, out_shape=(jax.ShapeDtypeStruct((tiles, 4, 2) + pi...  440 us
    pallas_call x1, Pallas kernels, step(): pl.pallas_call(adamw_kernel, out_shape=[jax.ShapeDtypeStruct(a.shape, a.d...  14.8 us

profile of v2, /device:TPU:0, one launch (start us, length us, event | category | flops | bytes accessed | tf_op | source)
XLA Modules:
  0.0 462.4 jit_solution(3598697138376666559)
XLA Ops:
  0.6 6.8 %pack.1.pk_hbm = bf16[16,3,64,512]{3,2,1,0:T(8,128)(2,1)} custom-call(bf16[2,64,4096]{2,1,0:T(8,128)(2,1)} %refs_0_.1, bf16[2,64,4096]{2,1,0:T(8,128)(2,1)} %refs_1_.1, bf16[2,8,64,512]{3,2,1,0:T(8,128)(2,1)} %bitcast.8), custom_call_target="tpu_custom_call" | custom-call | tf_op jit(solution)/shard_map/pack/pallas_call | solution.py:437
  7.4 440.1 %step.1 = (bf16[16,4,2,3,64,512]{5,4,3,2,1,0:T(8,128)(2,1)}, bf16[16,3,64,512]{3,2,1,0:T(8,128)(2,1)}) custom-call(bf16[4096,512]{1,0:T(8,128)(2,1)} %bitcast.12, bf16[4096,512]{1,0:T(8,128)(2,1)} %bitcast.13, bf16[16,3,64,512]{3,2,1,0:T(8,128)(2,1)} %pack.1.pk_hbm), custom_call_target="tpu_custom_call" | custom-call | flops 292057776128 | bytes 67108864 | tf_op jit(solution)/shard_map/step/pallas_call | solution.py:336
  447.5 14.8 %adamw.1 = (bf16[2,64,4096]{2,1,0:T(8,128)(2,1)}, bf16[2,64,4096]{2,1,0:T(8,128)(2,1)}, bf16[2,8,64,512]{3,2,1,0:T(8,128)(2,1)}, f32[2,64,4096]{2,1,0:T(8,128)},...) custom-call(bf16[16,3,64,512]{3,2,1,0:T(8,128)(2,1)} %get-tuple-elem, ...), custom_call_target="tpu_custom_call" | custom-call | tf_op jit(solution)/shard_map/adamw/pallas_call | solution.py:446

commit v3 on v2

--- a/solution.py
+++ b/solution.py
@@ -119,6 +119,12 @@
         acc[at] = jnp.zeros((CHUNK, d_model), F32)
 
     each_chunk(prepare_forward)
+    get_dy.wait()
+
+    def turn(at, to):
+        DYT[:, to] = DY[at].T
+
+    each_chunk(turn)
     pass_on(0)
     whole(0)
     load(0, 0)
@@ -142,7 +148,6 @@
 
     lax.fori_loop(0, half, forward, None)
     pass_on(half + 1)
-    get_dy.wait()
 
     def prepare_last(at, to):
         h = (H[at].astype(F32) + acc[at].astype(BF16).astype(F32)).astype(BF16)
@@ -151,7 +156,6 @@
         a = (wide * scale_of(wide)).astype(BF16)
         A[at] = a
         AT[:, to] = a.T
-        DYT[:, to] = DY[at].T
         acc[at] = jnp.zeros((CHUNK, d_model), F32)
 
     each_chunk(prepare_last)
@@ -423,7 +427,7 @@
     def step(x, dy, *arrays):
         layers, height, hidden = arrays[0].shape
         d_model = arrays[2].shape[2]
-        rows = 16
+        rows = 32
 
         def tiled(w):
             return w.reshape(layers, 8, height, d_model)

time: 463 us -> 457 us (0.987)
  Pallas kernels: 462 us -> 456 us
where the time goes in v3:
time: 457 us
  Pallas kernels  456 us (100%)
    pallas_call x1, Pallas kernels, gradients_of(): pl.pallas_call(kernel, out_shape=(jax.ShapeDtypeStruct((tiles, 4, 2) + pi...  439 us
    pallas_call x1, Pallas kernels, step(): pl.pallas_call(adamw_kernel, out_shape=[jax.ShapeDtypeStruct(a.shape, a.d...  12.6 us

profile of v3, /device:TPU:0, one launch (start us, length us, event | category | flops | bytes accessed | tf_op | source)
XLA Modules:
  0.0 456.9 jit_solution(11638010081967027926)
XLA Ops:
  0.6 4.6 %pack.1.pk_hbm = bf16[16,3,64,512]{3,2,1,0:T(8,128)(2,1)} custom-call(bf16[2,64,4096]{2,1,0:T(8,128)(2,1)} %refs_0_.1, bf16[2,64,4096]{2,1,0:T(8,128)(2,1)} %refs_1_.1, bf16[2,8,64,512]{3,2,1,0:T(8,128)(2,1)} %bitcast.8), custom_call_target="tpu_custom_call" | custom-call | tf_op jit(solution)/shard_map/pack/pallas_call | solution.py:441
  5.2 438.9 %step.1 = (bf16[16,4,2,3,64,512]{5,4,3,2,1,0:T(8,128)(2,1)}, bf16[16,3,64,512]{3,2,1,0:T(8,128)(2,1)}) custom-call(bf16[4096,512]{1,0:T(8,128)(2,1)} %bitcast.12, bf16[4096,512]{1,0:T(8,128)(2,1)} %bitcast.13, bf16[16,3,64,512]{3,2,1,0:T(8,128)(2,1)} %pack.1.pk_hbm), custom_call_target="tpu_custom_call" | custom-call | flops 292057776128 | bytes 67108864 | tf_op jit(solution)/shard_map/step/pallas_call | solution.py:340
  444.2 12.6 %adamw.1 = (bf16[2,64,4096]{2,1,0:T(8,128)(2,1)}, bf16[2,64,4096]{2,1,0:T(8,128)(2,1)}, bf16[2,8,64,512]{3,2,1,0:T(8,128)(2,1)}, f32[2,64,4096]{2,1,0:T(8,128)},...) custom-call(bf16[16,3,64,512]{3,2,1,0:T(8,128)(2,1)} %get-tuple-elem, ...), custom_call_target="tpu_custom_call" | custom-call | tf_op jit(solution)/shard_map/adamw/pallas_call | solution.py:450
